TPU v7x, 32 devices: a whole 2x2x4 slice. The times are simulated.
32 devices in a mesh: gx: 4 (over z), gy: 2 (over y), gz: 4 (over x, core).
Axes of the slice: x: 2, y: 2, z: 4, core: 2. Of those that a mesh axis runs over, the one named last changes fastest.
Arguments:
- cell_volume: float32 [64, 32, 512], P('gx', 'gy', 'gz'), may hold values from 0.5 to 2
- exponent: int32 [64, 32, 512], P('gx', 'gy', 'gz'), may hold values from 0 to 7
- owner_row: int32 [8192], P(('gx', 'gy', 'gz')), may hold values from 0 to 8191, as said below
Outputs:
- stencil_out: float32 [27, 8192, 128], P(None, ('gx', 'gy', 'gz'))
- lumped_out: float32 [8192, 128], P(('gx', 'gy', 'gz'))
Inputs may be any that keep to these rules, and one draw needn't show every extreme that they name: owner_row is a permutation of the row blocks; the row blocks of each device's share of owner_row go to each owner (owner_row // 256) exactly 8 times.
All inputs are finite; a program needn't handle non-finite values.
Results may differ from a plain program's by a relative error of at most 0.00007.
Values sent between devices are 32-bit elements; how exact they have to be, the bound alone decides.
A program may use at most 64 MiB of HBM per device.

v0:
```python
import jax
import jax.numpy as jnp
import numpy as np
from jax import lax
from jax.sharding import PartitionSpec as P

log_step = 0.3


def from_behind(block, axis, distance):
    devices = range(lax.axis_size(axis))
    route = [((i - distance) % len(devices), i) for i in devices]
    return lax.ppermute(block, axis, route)


def weight_table():
    table = np.zeros((27, 8), np.float32)
    for index_o in range(27):
        offsets = (index_o // 9 - 1, index_o // 3 % 3 - 1, index_o % 3 - 1)
        for index_a in range(8):
            corner = (index_a // 4, index_a // 2 % 2, index_a % 2)
            inside = all((0 <= corner[slot_d] + offsets[slot_d] <= 1 for slot_d in range(3)))
            factor = 1.0
            for slot_d in range(3):
                factor = factor * (2.0 if offsets[slot_d] == 0 else 1.0)
            table[index_o, index_a] = factor / 64.0 if inside else 0.0
    return table


def rim_section(current, along, stack_at, sender):
    length = current.shape[along]
    interior = lax.slice_in_dim(current, 0, length - 1, axis=along)
    top_layer = lax.slice_in_dim(current, length - 1, length, axis=along)
    received = sender(top_layer)
    behind = jnp.concatenate([received, interior], axis=along)
    return jnp.stack([current, behind], axis=stack_at)


def shards(cell_volume, exponent, owner_row):
    weight = cell_volume * jnp.exp(-log_step * exponent.astype(jnp.float32))
    span_x, span_y, span_z = weight.shape
    line_count = span_x * span_y
    devices_all = lax.axis_size(("gx", "gy", "gz"))

    def send_x(rim_layer):
        return from_behind(rim_layer, "gx", 1)

    def send_y(rim_layer):
        return from_behind(rim_layer, "gy", 1)

    owner_dev = owner_row // line_count
    by_owner = jnp.argsort(owner_dev, stable=True)
    slot_ids = (owner_row % line_count)[by_owner].reshape(1, devices_all, -1)
    table = jnp.asarray(weight_table())
    sectioned_x = rim_section(weight, 0, 0, send_x)
    sectioned_xy = rim_section(sectioned_x, 2, 1, send_y)
    lines = sectioned_xy.reshape(4, line_count, span_z)
    rim_values = from_behind(sectioned_xy[..., span_z - 1 :], "gz", 1).reshape(4, line_count)
    packed = lines[:, by_owner].reshape(4, devices_all, -1, span_z)
    rim_packed = rim_values[:, by_owner].reshape(4, devices_all, -1)
    got_lines, got_rims, got_slots = (
        lax.all_to_all(packed, ("gx", "gy", "gz"), split_axis=1, concat_axis=1, tiled=True),
        lax.all_to_all(rim_packed, ("gx", "gy", "gz"), split_axis=1, concat_axis=1, tiled=True),
        lax.all_to_all(slot_ids, ("gx", "gy", "gz"), split_axis=1, concat_axis=1, tiled=True),
    )
    placing = jnp.argsort(got_slots.reshape(-1))
    current = got_lines.reshape(4, line_count, span_z)[:, placing]
    before = got_rims.reshape(4, line_count)[:, placing]
    behind = jnp.concatenate([before[..., None], current[..., : span_z - 1]], axis=2)
    corners = jnp.stack([current, behind], axis=1).reshape(8, line_count, span_z)
    stencil_rows = jnp.einsum("oa,alz->olz", table, corners, precision=lax.Precision.HIGHEST)
    lumped_rows = 1.0 / jnp.sum(stencil_rows, axis=0)
    return (stencil_rows, lumped_rows)


def solution(mesh):
    return jax.shard_map(
        shards,
        mesh=mesh,
        in_specs=(P("gx", "gy", "gz"), P("gx", "gy", "gz"), P(("gx", "gy", "gz"))),
        out_specs=(P(None, ("gx", "gy", "gz"), None), P(("gx", "gy", "gz"), None)),
        check_vma=False,
    )
```

profile of v0, /device:TPU:0, one launch (start us, length us, event | category | flops | bytes accessed | tf_op | source)
XLA Modules:
  0.0 66.7 jit_solution(13630262406832950411)
XLA Ops:
  0.6 1.0 %exponential_multiply_fusion = f32[16,16,128]{2,1,0:T(8,128)S(1)} fusion(f32[16,16,128]{2,1,0:T(8,128)} %param.4, s32[16,16,128]{2,1,0:T(8,128)} %param.5), kind=kLoop, calls=%fused_computation.20 | loop fusion | flops 98304 | bytes 393216 | tf_op jit(solution)/shard_map/mul | solution.py:40
  1.6 3.1 %collective-permute-start = (f32[1,16,128]{2,1,0:T(8,128)S(1)}, f32[1,16,128]{2,1,0:T(8,128)S(1)}, u32[]{:S(2)}, u32[]{:S(2)}) collective-permute-start(f32[1,16,128]{2,1,0:T(8,128)S(1)} %slice.34), channel_id=1, source_target_pairs={{24,0},{0,8},{8,16},{16,24},{25,1},{1,9},{9,17},{17,25},{26,2},{2,... | collective-permute-start | bytes 24584 | tf_op jit(solution)/shard_map/ppermute | solution.py:13
  4.7 0.7 %and_select_fusion = (s32[256]{0:T(256)S(1)}, s32[256]{0:T(256)S(1)}) fusion(s32[256]{0:T(256)} %param.6), kind=kLoop, calls=%fused_computation.27 | loop fusion | flops 4864 | bytes 3072 | tf_op jit(solution)/shard_map/jit(remainder)/select_n | solution.py:53
  5.4 3.2 %sort.34 = (s32[256]{0:T(256)}, s32[256]{0:T(256)S(1)}) sort(s32[256]{0:T(256)S(1)} %get-tuple-element.15, s32[256]{0:T(256)S(1)} %iota.8), dimensions={0}, to_apply=%region_0.1 | sort | flops 2048 | bytes 4096 | tf_op jit(solution)/shard_map/jit(argsort)/sort | solution.py:52
  8.6 0.0 collective-permute-done
  8.7 1.6 %collective-permute-start.1 = (f32[2,16,1,128]{3,2,1,0:T(1,128)S(1)}, f32[2,16,1,128]{3,2,1,0:T(1,128)S(1)}, u32[]{:S(2)}, u32[]{:S(2)}) collective-permute-start(f32[2,16,1,128]{3,2,1,0:T(1,128)S(1)} %fusion.3), channel_id=1, source_target_pairs={{4,0},{0,4},{5,1},{1,5},{6,2},{2,6},{7,3},{3,7},{12,8},{8,12},{13,... | collective-permute-start | bytes 49160 | tf_op jit(solution)/shard_map/ppermute | solution.py:13
  10.3 2.2 %collective-permute-done.1 = f32[2,16,1,128]{3,2,1,0:T(1,128)S(1)} collective-permute-done((f32[2,16,1,128]{3,2,1,0:T(1,128)S(1)}, f32[2,16,1,128]{3,2,1,0:T(1,128)S(1)}, u32[]{:S(2)}, u32[]{:S(2)}) %collective-permute-start.1) | collective-permute-done | bytes 16416 | tf_op jit(solution)/shard_map/ppermute | solution.py:13
  12.5 0.2 fusion
  12.7 0.1 collective-permute-start.2
  12.8 1.9 %gather_fusion.1 = s32[256]{0:T(256)S(1)} fusion(s32[256]{0:T(256)S(1)} %get-tuple-element.14, s32[1024]{0:T(1024)S(1)} %pad_clamp_fusion.1), kind=kCustom, calls=%fused_computation.1 | custom fusion | bytes 3072 | tf_op jit(solution)/shard_map/gather | solution.py:53
  14.8 0.7 %reshape.34 = s32[1,32,8]{2,1,0:T(8,128)} reshape(s32[256]{0:T(256)S(1)} %gather_fusion.1) | data formatting | bytes 2048 | tf_op jit(solution)/shard_map/reshape | solution.py:53
  15.5 5.1 %all-to-all-start.1 = ((s32[1,32,8]{2,0,1:T(1,128)}), s32[1,32,8]{2,0,1:T(1,128)S(1)}, u32[]{:S(2)}, u32[]{:S(2)}) async-start(s32[1,32,8]{2,0,1:T(1,128)} %bitcast.10), calls=%async_computation.1 | async-start | bytes 32768 | tf_op jit(solution)/shard_map/all_to_all | solution.py:64
  20.6 0.8 %collective-permute-done.2 = f32[2,2,16,16,1]{4,3,2,1,0:T(8,128)S(1)} collective-permute-done((f32[2,2,16,16,1]{4,3,2,1,0:T(8,128)S(1)}, f32[2,2,16,16,1]{4,3,2,1,0:T(8,128)S(1)}, u32[]{:S(2)}, u32[]{:S(2)}) %collective-permute-start.2) | collective-permute-done | bytes 4128 | tf_op jit(solution)/shard_map/ppermute | solution.py:13
  21.4 0.2 reduce.1
  21.6 0.1 reshape.36
  21.7 0.1 copy.25
  21.8 0.7 %gather_fusion.3 = f32[256,4]{1,0:T(8,128)S(1)} fusion(f32[4,256]{0,1:T(8,128)S(1)} %copy.25, s32[1024]{0:T(1024)S(1)} %pad_clamp_fusion.1), kind=kCustom, calls=%fused_computation.3 | custom fusion | bytes 9216 | tf_op jit(solution)/shard_map/gather | solution.py:60
  22.6 0.9 %copy.26 = f32[4,32,8]{2,0,1:T(4,128)} copy(f32[4,32,8]{0,2,1:T(8,128)S(1)} %bitcast.45) | data formatting | bytes 8192 | tf_op jit(solution)/shard_map/reshape | solution.py:60
  23.5 4.2 %all-to-all-done.1 = s32[1,32,8]{2,0,1:T(1,128)S(1)} async-done(((s32[1,32,8]{2,0,1:T(1,128)}), s32[1,32,8]{2,0,1:T(1,128)S(1)}, u32[]{:S(2)}, u32[]{:S(2)}) %all-to-all-start.1) | async-done | bytes 1056 | tf_op jit(solution)/shard_map/all_to_all | solution.py:64
  27.7 2.6 %all-to-all-start.2 = ((f32[4,32,8]{2,0,1:T(4,128)}), f32[4,32,8]{2,0,1:T(4,128)S(1)}, u32[]{:S(2)}, u32[]{:S(2)}) async-start(f32[4,32,8]{2,0,1:T(4,128)} %copy.26), calls=%async_computation.2 | async-start | bytes 131072 | tf_op jit(solution)/shard_map/all_to_all | solution.py:63
  30.3 0.3 copy.23
  30.7 1.8 %gather_fusion = f32[256,4,128]{2,1,0:T(4,128)} fusion(f32[4,256,128]{2,0,1:T(4,128)S(1)} %copy.23, s32[1024]{0:T(1024)S(1)} %pad_clamp_fusion.1), kind=kCustom, calls=%fused_computation | custom fusion | bytes 1049600 | tf_op jit(solution)/shard_map/gather | solution.py:59
  32.4 5.3 %all-to-all-done.2 = f32[4,32,8]{2,0,1:T(4,128)S(1)} async-done(((f32[4,32,8]{2,0,1:T(4,128)}), f32[4,32,8]{2,0,1:T(4,128)S(1)}, u32[]{:S(2)}, u32[]{:S(2)}) %all-to-all-start.2) | async-done | bytes 4128 | tf_op jit(solution)/shard_map/all_to_all | solution.py:63
  37.7 0.0 copy-start
  37.7 2.9 %all-to-all-start = ((f32[4,32,8,128]{3,0,2,1:T(4,128)}), f32[4,32,8,128]{3,0,2,1:T(4,128)S(1)}, u32[]{:S(2)}, u32[]{:S(2)}) async-start(f32[4,32,8,128]{3,0,2,1:T(4,128)} %bitcast.8), calls=%async_computation | async-start | bytes 1048576 | tf_op jit(solution)/shard_map/all_to_all | solution.py:62
  40.6 0.5 broadcast.55
  41.1 0.7 %reduce.4 = s32[32,8]{1,0:T(8,128)S(1)} reduce(s32[1,32,8]{2,0,1:T(1,128)S(1)} %all-to-all-done.1, s32[]{:T(128)} %broadcast.55), dimensions={0}, to_apply=%all_to_all.10.reduce_sub_computation.3 | reduce | bytes 2052 | tf_op jit(solution)/shard_map/all_to_all | solution.py:64
  41.8 0.1 reshape.35
  41.9 3.2 %sort.35 = (s32[256]{0:T(256)}, s32[256]{0:T(256)S(1)}) sort(s32[256]{0:T(256)S(1)} %reshape.35, s32[256]{0:T(256)S(1)} %iota.9), dimensions={0}, to_apply=%region_1.2 | sort | flops 2048 | bytes 4096 | tf_op jit(solution)/shard_map/jit(argsort)/sort | solution.py:66
  45.1 0.3 copy.27
  45.3 0.7 %gather_fusion.4 = f32[256,4]{1,0:T(8,128)S(1)} fusion(f32[4,256]{0,1:T(8,128)S(1)} %bitcast.43, s32[1024]{0:T(1024)S(1)} %pad_clamp_fusion), kind=kCustom, calls=%fused_computation.4 | custom fusion | bytes 9216 | tf_op jit(solution)/shard_map/gather | solution.py:68
  46.1 1.7 %copy.29 = f32[4,256,1]{2,0,1:T(4,128)S(1)} copy(f32[4,256,1]{0,1,2:T(8,128)S(1)} %bitcast.44) | data formatting | bytes 8192 | tf_op jit(solution)/shard_map/broadcast_in_dim | solution.py:69
  47.7 8.3 %all-to-all-done = f32[4,32,8,128]{3,0,2,1:T(4,128)S(1)} async-done(((f32[4,32,8,128]{3,0,2,1:T(4,128)}), f32[4,32,8,128]{3,0,2,1:T(4,128)S(1)}, u32[]{:S(2)}, u32[]{:S(2)}) %all-to-all-start) | async-done | bytes 524320 | tf_op jit(solution)/shard_map/all_to_all | solution.py:62
  56.0 1.0 %gather_fusion.2 = f32[256,4,128]{2,1,0:T(4,128)S(1)} fusion(f32[4,256,128]{2,0,1:T(4,128)S(1)} %bitcast.41, s32[1024]{0:T(1024)S(1)} %pad_clamp_fusion), kind=kCustom, calls=%fused_computation.2 | custom fusion | bytes 1049600 | tf_op jit(solution)/shard_map/gather | solution.py:67
  57.0 0.3 maximum_bitcast_fusion
  57.4 0.2 pad_maximum_fusion
  57.6 0.8 %copy.30 = f32[4,2,256,128]{3,1,0,2:T(2,128)S(1)} copy(f32[4,2,256,128]{3,0,2,1:T(4,128)S(1)} %pad_maximum_fusion) | data formatting | bytes 2097152 | tf_op jit(solution)/shard_map/stack | solution.py:70
  58.4 0.0 copy-done
  58.4 3.7 %fusion.4 = (f32[256,128]{1,0:T(8,128)S(1)}, f32[27,256,128]{2,0,1:T(8,128)S(1)}) fusion(f32[27,8,1]{0,1,2:T(8,128)S(1)} %copy-done, f32[8,256,128]{2,0,1:T(8,128)S(1)} %bitcast.37), kind=kOutput, calls=%fused_computation.34 | convolution fusion | flops 85786624 | bytes 4719456 | tf_op jit(solution)/shard_map/oa,alz->olz/dot_general | solution.py:71
  62.2 0.7 %broadcast_divide_fusion = f32[256,128]{1,0:T(8,128)} fusion(f32[256,128]{1,0:T(8,128)S(1)} %get-tuple-element.16), kind=kLoop, calls=%fused_computation.21 | loop fusion | flops 32768 | bytes 262144 | tf_op jit(solution)/shard_map/div | solution.py:72
  62.8 3.8 %copy.31 = f32[27,256,128]{2,1,0:T(8,128)} copy(f32[27,256,128]{2,0,1:T(8,128)S(1)} %get-tuple-element.17) | data formatting | bytes 7077888
  (14 shorter events, 0.2 us)
Async XLA Ops:
  1.6 7.0 %collective-permute-start = (f32[1,16,128]{2,1,0:T(8,128)S(1)}, f32[1,16,128]{2,1,0:T(8,128)S(1)}, u32[]{:S(2)}, u32[]{:S(2)}) collective-permute-start(f32[1,16,128]{2,1,0:T(8,128)S(1)} %slice.34), channel_id=1, source_target_pairs={{24,0},{0,8},{8,16},{16,24},{25,1},{1,9},{9,17},{17,25},{26,2},{2,... | collective-permute-start | bytes 24584 | tf_op jit(solution)/shard_map/ppermute | solution.py:13
  8.7 3.8 %collective-permute-start.1 = (f32[2,16,1,128]{3,2,1,0:T(1,128)S(1)}, f32[2,16,1,128]{3,2,1,0:T(1,128)S(1)}, u32[]{:S(2)}, u32[]{:S(2)}) collective-permute-start(f32[2,16,1,128]{3,2,1,0:T(1,128)S(1)} %fusion.3), channel_id=1, source_target_pairs={{4,0},{0,4},{5,1},{1,5},{6,2},{2,6},{7,3},{3,7},{12,8},{8,12},{13,... | collective-permute-start | bytes 49160 | tf_op jit(solution)/shard_map/ppermute | solution.py:13
  12.7 8.7 %collective-permute-start.2 = (f32[2,2,16,16,1]{4,3,2,1,0:T(8,128)S(1)}, f32[2,2,16,16,1]{4,3,2,1,0:T(8,128)S(1)}, u32[]{:S(2)}, u32[]{:S(2)}) collective-permute-start(f32[2,2,16,16,1]{4,3,2,1,0:T(8,128)S(1)} %fusion), channel_id=1, source_target_pairs={{3,0},{0,1},{1,2},{2,3},{7,4},{4,5},{5,6},{6,7},{11,8},{8,9},{9,10... | collective-permute-start | bytes 12296 | tf_op jit(solution)/shard_map/ppermute | solution.py:13
  15.5 12.2 %all-to-all-start.1 = ((s32[1,32,8]{2,0,1:T(1,128)}), s32[1,32,8]{2,0,1:T(1,128)S(1)}, u32[]{:S(2)}, u32[]{:S(2)}) async-start(s32[1,32,8]{2,0,1:T(1,128)} %bitcast.10), calls=%async_computation.1 | async-start | bytes 32768 | tf_op jit(solution)/shard_map/all_to_all | solution.py:64
  27.7 10.0 %all-to-all-start.2 = ((f32[4,32,8]{2,0,1:T(4,128)}), f32[4,32,8]{2,0,1:T(4,128)S(1)}, u32[]{:S(2)}, u32[]{:S(2)}) async-start(f32[4,32,8]{2,0,1:T(4,128)} %copy.26), calls=%async_computation.2 | async-start | bytes 131072 | tf_op jit(solution)/shard_map/all_to_all | solution.py:63
  37.7 20.8 %copy-start = (f32[27,8,1]{0,1,2:T(8,128)S(1)}, f32[27,8,1]{0,1,2:T(8,128)}, u32[]{:S(2)}) copy-start(f32[27,8,1]{0,1,2:T(8,128)} %constant.39) | copy-start | bytes 2596
  37.7 18.4 %all-to-all-start = ((f32[4,32,8,128]{3,0,2,1:T(4,128)}), f32[4,32,8,128]{3,0,2,1:T(4,128)S(1)}, u32[]{:S(2)}, u32[]{:S(2)}) async-start(f32[4,32,8,128]{3,0,2,1:T(4,128)} %bitcast.8), calls=%async_computation | async-start | bytes 1048576 | tf_op jit(solution)/shard_map/all_to_all | solution.py:62
where the time goes:
time: 67 us; the launch traced here: 66.7 us
  waiting for transfers between devices  20.8 us (31%)
  local copies, waits for them, and re-layouts  15.5 us (23%)
  starting transfers between devices  15.3 us (23%)
  other arithmetic  10.5 us (16%)
  matrix products  3.72 us (6%)
  between operations  0.83 us (1%)
    all_to_all x1, waiting for transfers between devices, shards(): lax.all_to_all(packed, ('gx', 'gy', 'gz'), split_axis=1, concat_axis=1, t...  8.3 us
    all_to_all x1, waiting for transfers between devices, shards(): lax.all_to_all(rim_packed, ('gx', 'gy', 'gz'), split_axis=1, concat_axis=...  5.26 us
    all_to_all x1, starting transfers between devices, shards(): lax.all_to_all(slot_ids, ('gx', 'gy', 'gz'), split_axis=1, concat_axis=1,...  5.1 us
    ppermute x3, starting transfers between devices, from_behind(): return lax.ppermute(block, axis, route)  4.74 us
    all_to_all x1, waiting for transfers between devices, shards(): lax.all_to_all(slot_ids, ('gx', 'gy', 'gz'), split_axis=1, concat_axis=1,...  4.21 us
    unnamed x3, local copies, waits for them, and re-layouts  3.85 us
    dot_general x1, matrix products, shards(): jnp.einsum('oa,alz->olz', table, corners, precision=lax.Precision.HIGHEST)  3.72 us
    sort x1, other arithmetic, shards(): by_owner = jnp.argsort(owner_dev, stable=True)  3.17 us
  transfers between devices with their start and end apart: 6, of which 5 were waited for; matrix products, arithmetic and copies ran while one was open for 27% of the time, Pallas kernels for 0%

commit v1 on v0

--- a/solution.py
+++ b/solution.py
@@ -3,6 +3,7 @@
 import numpy as np
 from jax import lax
 from jax.sharding import PartitionSpec as P
+from jax.lax import all_to_all, axis_size
 
 log_step = 0.3
 
@@ -58,10 +59,17 @@
     rim_values = from_behind(sectioned_xy[..., span_z - 1 :], "gz", 1).reshape(4, line_count)
     packed = lines[:, by_owner].reshape(4, devices_all, -1, span_z)
     rim_packed = rim_values[:, by_owner].reshape(4, devices_all, -1)
+
+    def weights_drive(target, row_axis):
+        return jnp.concatenate(
+            all_to_all(jnp.stack(jnp.split(target, axis_size(row_axis), axis=1)), row_axis, 0, 0),
+            axis=1,
+        )
+
     got_lines, got_rims, got_slots = (
         lax.all_to_all(packed, ("gx", "gy", "gz"), split_axis=1, concat_axis=1, tiled=True),
         lax.all_to_all(rim_packed, ("gx", "gy", "gz"), split_axis=1, concat_axis=1, tiled=True),
-        lax.all_to_all(slot_ids, ("gx", "gy", "gz"), split_axis=1, concat_axis=1, tiled=True),
+        weights_drive(slot_ids, ("gx", "gy", "gz")),
     )
     placing = jnp.argsort(got_slots.reshape(-1))
     current = got_lines.reshape(4, line_count, span_z)[:, placing]

time: 67 us -> 83.2 us (1.24)
  local copies, waits for them, and re-layouts: 15.5 us -> 31.3 us
    unnamed x3 -> x34, local copies, waits for them, and re-layouts: 3.85 us -> 19.7 us
    ppermute x3, waiting for transfers between devices: 3.03 us -> 5.16 us  [from_behind(): return lax.ppermute(block, axis, route)]
    all_to_all x1, waiting for transfers between devices: 4.21 us -> 2.07 us  [weights_drive(): all_to_all(jnp.stack(jnp.split(target, axis_size(row_axis), axis=1)), row...]
  transfers between devices with their start and end apart: 6 -> 6, of which waited for: 5 -> 5; matrix products, arithmetic and copies ran while one was open for 27% -> 41% of each run, Pallas kernels for 0% -> 0%
where the time goes in v1:
time: 83.2 us; the launch traced here: 82.8 us
  local copies, waits for them, and re-layouts  31.3 us (38%)
  waiting for transfers between devices  20.8 us (25%)
  starting transfers between devices  15.7 us (19%)
  other arithmetic  10.5 us (13%)
  matrix products  3.72 us (4%)
  between operations  0.84 us (1%)
    unnamed x34, local copies, waits for them, and re-layouts  19.7 us
    all_to_all x1, waiting for transfers between devices, shards(): lax.all_to_all(packed, ('gx', 'gy', 'gz'), split_axis=1, concat_axis=1, t...  8.3 us
    all_to_all x1, waiting for transfers between devices, shards(): lax.all_to_all(rim_packed, ('gx', 'gy', 'gz'), split_axis=1, concat_axis=...  5.26 us
    ppermute x3, waiting for transfers between devices, from_behind(): return lax.ppermute(block, axis, route)  5.16 us
    all_to_all x1, starting transfers between devices, weights_drive(): all_to_all(jnp.stack(jnp.split(target, axis_size(row_axis), axis=1)), row...  5.1 us
    ppermute x3, starting transfers between devices, from_behind(): return lax.ppermute(block, axis, route)  4.74 us
    dot_general x1, matrix products, shards(): jnp.einsum('oa,alz->olz', table, corners, precision=lax.Precision.HIGHEST)  3.72 us
    sort x1, other arithmetic, shards(): by_owner = jnp.argsort(owner_dev, stable=True)  3.17 us
  transfers between devices with their start and end apart: 6, of which 5 were waited for; matrix products, arithmetic and copies ran while one was open for 41% of the time, Pallas kernels for 0%

profile of v1, /device:TPU:0, one launch (start us, length us, event | category | flops | bytes accessed | tf_op | source)
XLA Modules:
  0.0 82.8 jit_solution(1770591275847221731)
XLA Ops:
  0.6 1.0 %exponential_multiply_fusion = f32[16,16,128]{2,1,0:T(8,128)S(1)} fusion(f32[16,16,128]{2,1,0:T(8,128)} %param.4, s32[16,16,128]{2,1,0:T(8,128)} %param.5), kind=kLoop, calls=%fused_computation.20 | loop fusion | flops 98304 | bytes 393216 | tf_op jit(solution)/shard_map/mul | solution.py:41
  1.6 3.1 %collective-permute-start = (f32[1,16,128]{2,1,0:T(8,128)S(1)}, f32[1,16,128]{2,1,0:T(8,128)S(1)}, u32[]{:S(2)}, u32[]{:S(2)}) collective-permute-start(f32[1,16,128]{2,1,0:T(8,128)S(1)} %slice.34), channel_id=1, source_target_pairs={{24,0},{0,8},{8,16},{16,24},{25,1},{1,9},{9,17},{17,25},{26,2},{2,... | collective-permute-start | bytes 24584 | tf_op jit(solution)/shard_map/ppermute | solution.py:14
  4.7 0.7 and_select_fusion
  5.4 3.2 %sort.34 = (s32[256]{0:T(256)}, s32[256]{0:T(256)S(1)}) sort(s32[256]{0:T(256)S(1)} %get-tuple-element.19, s32[256]{0:T(256)S(1)} %iota.8), dimensions={0}, to_apply=%region_0.1 | sort | flops 2048 | bytes 4096 | tf_op jit(solution)/shard_map/jit(argsort)/sort | solution.py:53
  8.6 1.9 %gather_fusion.1 = s32[256]{0:T(256)S(1)} fusion(s32[256]{0:T(256)S(1)} %get-tuple-element.18, s32[1024]{0:T(1024)S(1)} %pad_clamp_fusion.1), kind=kCustom, calls=%fused_computation.1 | custom fusion | bytes 3072 | tf_op jit(solution)/shard_map/gather | solution.py:54
  10.6 0.5 constant_dynamic-update-slice_fusion.31
  11.2 0.5 constant_dynamic-update-slice_fusion.30
  11.7 0.5 constant_dynamic-update-slice_fusion.29
  12.2 0.5 constant_dynamic-update-slice_fusion.28
  12.7 0.5 constant_dynamic-update-slice_fusion.27
  14.2 0.5 constant_dynamic-update-slice_fusion.24
  15.3 0.5 constant_dynamic-update-slice_fusion.22
  15.8 0.5 constant_dynamic-update-slice_fusion.21
  16.3 0.5 constant_dynamic-update-slice_fusion.20
  16.8 0.5 constant_dynamic-update-slice_fusion.19
  19.4 0.5 constant_dynamic-update-slice_fusion.14
  19.9 0.5 constant_dynamic-update-slice_fusion.13
  20.4 0.5 constant_dynamic-update-slice_fusion.12
  20.9 0.5 constant_dynamic-update-slice_fusion.11
  21.4 0.5 constant_dynamic-update-slice_fusion.10
  21.9 0.5 constant_dynamic-update-slice_fusion.9
  24.5 0.5 constant_dynamic-update-slice_fusion.4
  25.0 0.5 constant_dynamic-update-slice_fusion.3
  25.5 0.5 constant_dynamic-update-slice_fusion.2
  26.0 0.5 constant_dynamic-update-slice_fusion.1
  26.7 1.6 %collective-permute-start.1 = (f32[2,16,1,128]{3,2,1,0:T(1,128)S(1)}, f32[2,16,1,128]{3,2,1,0:T(1,128)S(1)}, u32[]{:S(2)}, u32[]{:S(2)}) collective-permute-start(f32[2,16,1,128]{3,2,1,0:T(1,128)S(1)} %fusion.3), channel_id=1, source_target_pairs={{4,0},{0,4},{5,1},{1,5},{6,2},{2,6},{7,3},{3,7},{12,8},{8,12},{13,... | collective-permute-start | bytes 49160 | tf_op jit(solution)/shard_map/ppermute | solution.py:14
  28.3 2.2 %collective-permute-done.1 = f32[2,16,1,128]{3,2,1,0:T(1,128)S(1)} collective-permute-done((f32[2,16,1,128]{3,2,1,0:T(1,128)S(1)}, f32[2,16,1,128]{3,2,1,0:T(1,128)S(1)}, u32[]{:S(2)}, u32[]{:S(2)}) %collective-permute-start.1) | collective-permute-done | bytes 16416 | tf_op jit(solution)/shard_map/ppermute | solution.py:14
  30.8 0.5 constant_dynamic-update-slice_fusion
  31.3 5.1 %all-to-all-start.1 = ((s32[32,1,1,8]{3,2,1,0:T(1,128)}), s32[32,1,1,8]{3,2,1,0:T(1,128)S(1)}, u32[]{:S(2)}, u32[]{:S(2)}) async-start(s32[32,1,1,8]{3,2,1,0:T(1,128)} %constant_dynamic-update-slice_fusion), calls=%async_computation.1 | async-start | bytes 32768 | tf_op jit(solution)/shard_map/all_to_all | solution.py:65
  36.4 3.0 %collective-permute-done.2 = f32[2,2,16,16,1]{4,3,2,1,0:T(8,128)S(1)} collective-permute-done((f32[2,2,16,16,1]{4,3,2,1,0:T(8,128)S(1)}, f32[2,2,16,16,1]{4,3,2,1,0:T(8,128)S(1)}, u32[]{:S(2)}, u32[]{:S(2)}) %collective-permute-start.2) | collective-permute-done | bytes 4128 | tf_op jit(solution)/shard_map/ppermute | solution.py:14
  39.8 0.7 gather_fusion.3
  40.5 0.9 %copy.109 = f32[4,32,8]{2,0,1:T(4,128)} copy(f32[4,32,8]{0,2,1:T(8,128)S(1)} %bitcast.171) | data formatting | bytes 8192 | tf_op jit(solution)/shard_map/reshape | solution.py:61
  41.4 2.1 %all-to-all-done.1 = s32[32,1,1,8]{3,2,1,0:T(1,128)S(1)} async-done(((s32[32,1,1,8]{3,2,1,0:T(1,128)}), s32[32,1,1,8]{3,2,1,0:T(1,128)S(1)}, u32[]{:S(2)}, u32[]{:S(2)}) %all-to-all-start.1) | async-done | bytes 1056 | tf_op jit(solution)/shard_map/all_to_all | solution.py:65
  43.5 2.9 %all-to-all-start.2 = ((f32[4,32,8]{2,0,1:T(4,128)}), f32[4,32,8]{2,0,1:T(4,128)S(1)}, u32[]{:S(2)}, u32[]{:S(2)}) async-start(f32[4,32,8]{2,0,1:T(4,128)} %copy.109), calls=%async_computation.2 | async-start | bytes 131072 | tf_op jit(solution)/shard_map/all_to_all | solution.py:71
  46.8 1.8 %gather_fusion = f32[256,4,128]{2,1,0:T(4,128)} fusion(f32[4,256,128]{2,0,1:T(4,128)S(1)} %copy.107, s32[1024]{0:T(1024)S(1)} %pad_clamp_fusion.1), kind=kCustom, calls=%fused_computation | custom fusion | bytes 1049600 | tf_op jit(solution)/shard_map/gather | solution.py:60
  48.6 5.3 %all-to-all-done.2 = f32[4,32,8]{2,0,1:T(4,128)S(1)} async-done(((f32[4,32,8]{2,0,1:T(4,128)}), f32[4,32,8]{2,0,1:T(4,128)S(1)}, u32[]{:S(2)}, u32[]{:S(2)}) %all-to-all-start.2) | async-done | bytes 4128 | tf_op jit(solution)/shard_map/all_to_all | solution.py:71
  53.8 2.9 %all-to-all-start = ((f32[4,32,8,128]{3,0,2,1:T(4,128)}), f32[4,32,8,128]{3,0,2,1:T(4,128)S(1)}, u32[]{:S(2)}, u32[]{:S(2)}) async-start(f32[4,32,8,128]{3,0,2,1:T(4,128)} %bitcast.8), calls=%async_computation | async-start | bytes 1048576 | tf_op jit(solution)/shard_map/all_to_all | solution.py:70
  56.7 0.5 broadcast.55
  57.3 0.7 reduce.4
  58.1 3.2 %sort.35 = (s32[256]{0:T(256)}, s32[256]{0:T(256)S(1)}) sort(s32[256]{0:T(256)S(1)} %reshape_reshape.3, s32[256]{0:T(256)S(1)} %iota.9), dimensions={0}, to_apply=%region_1.2 | sort | flops 2048 | bytes 4096 | tf_op jit(solution)/shard_map/jit(argsort)/sort | solution.py:74
  61.5 0.7 gather_fusion.4
  62.2 1.7 %copy.112 = f32[4,256,1]{2,0,1:T(4,128)S(1)} copy(f32[4,256,1]{0,1,2:T(8,128)S(1)} %bitcast.170) | data formatting | bytes 8192 | tf_op jit(solution)/shard_map/broadcast_in_dim | solution.py:77
  63.9 8.3 %all-to-all-done = f32[4,32,8,128]{3,0,2,1:T(4,128)S(1)} async-done(((f32[4,32,8,128]{3,0,2,1:T(4,128)}), f32[4,32,8,128]{3,0,2,1:T(4,128)S(1)}, u32[]{:S(2)}, u32[]{:S(2)}) %all-to-all-start) | async-done | bytes 524320 | tf_op jit(solution)/shard_map/all_to_all | solution.py:70
  72.2 1.0 %gather_fusion.2 = f32[256,4,128]{2,1,0:T(4,128)S(1)} fusion(f32[4,256,128]{2,0,1:T(4,128)S(1)} %bitcast.167, s32[1024]{0:T(1024)S(1)} %pad_clamp_fusion), kind=kCustom, calls=%fused_computation.2 | custom fusion | bytes 1049600 | tf_op jit(solution)/shard_map/gather | solution.py:75
  73.8 0.8 copy.113
  74.6 3.7 %fusion.4 = (f32[256,128]{1,0:T(8,128)S(1)}, f32[27,256,128]{2,0,1:T(8,128)S(1)}) fusion(f32[27,8,1]{0,1,2:T(8,128)S(1)} %copy-done, f32[8,256,128]{2,0,1:T(8,128)S(1)} %bitcast.163), kind=kOutput, calls=%fused_computation.98 | convolution fusion | flops 85786624 | bytes 4719456 | tf_op jit(solution)/shard_map/oa,alz->olz/dot_general | solution.py:79
  78.3 0.7 broadcast_divide_fusion
  79.0 3.8 %copy.114 = f32[27,256,128]{2,1,0:T(8,128)} copy(f32[27,256,128]{2,0,1:T(8,128)S(1)} %get-tuple-element.21) | data formatting | bytes 7077888
  (39 shorter events, 7.8 us)
Async XLA Ops:
  1.6 24.9 %collective-permute-start = (f32[1,16,128]{2,1,0:T(8,128)S(1)}, f32[1,16,128]{2,1,0:T(8,128)S(1)}, u32[]{:S(2)}, u32[]{:S(2)}) collective-permute-start(f32[1,16,128]{2,1,0:T(8,128)S(1)} %slice.34), channel_id=1, source_target_pairs={{24,0},{0,8},{8,16},{16,24},{25,1},{1,9},{9,17},{17,25},{26,2},{2,... | collective-permute-start | bytes 24584 | tf_op jit(solution)/shard_map/ppermute | solution.py:14
  26.7 3.8 %collective-permute-start.1 = (f32[2,16,1,128]{3,2,1,0:T(1,128)S(1)}, f32[2,16,1,128]{3,2,1,0:T(1,128)S(1)}, u32[]{:S(2)}, u32[]{:S(2)}) collective-permute-start(f32[2,16,1,128]{3,2,1,0:T(1,128)S(1)} %fusion.3), channel_id=1, source_target_pairs={{4,0},{0,4},{5,1},{1,5},{6,2},{2,6},{7,3},{3,7},{12,8},{8,12},{13,... | collective-permute-start | bytes 49160 | tf_op jit(solution)/shard_map/ppermute | solution.py:14
  30.7 8.7 %collective-permute-start.2 = (f32[2,2,16,16,1]{4,3,2,1,0:T(8,128)S(1)}, f32[2,2,16,16,1]{4,3,2,1,0:T(8,128)S(1)}, u32[]{:S(2)}, u32[]{:S(2)}) collective-permute-start(f32[2,2,16,16,1]{4,3,2,1,0:T(8,128)S(1)} %fusion), channel_id=1, source_target_pairs={{3,0},{0,1},{1,2},{2,3},{7,4},{4,5},{5,6},{6,7},{11,8},{8,9},{9,10... | collective-permute-start | bytes 12296 | tf_op jit(solution)/shard_map/ppermute | solution.py:14
  31.3 12.2 %all-to-all-start.1 = ((s32[32,1,1,8]{3,2,1,0:T(1,128)}), s32[32,1,1,8]{3,2,1,0:T(1,128)S(1)}, u32[]{:S(2)}, u32[]{:S(2)}) async-start(s32[32,1,1,8]{3,2,1,0:T(1,128)} %constant_dynamic-update-slice_fusion), calls=%async_computation.1 | async-start | bytes 32768 | tf_op jit(solution)/shard_map/all_to_all | solution.py:65
  43.5 10.3 %all-to-all-start.2 = ((f32[4,32,8]{2,0,1:T(4,128)}), f32[4,32,8]{2,0,1:T(4,128)S(1)}, u32[]{:S(2)}, u32[]{:S(2)}) async-start(f32[4,32,8]{2,0,1:T(4,128)} %copy.109), calls=%async_computation.2 | async-start | bytes 131072 | tf_op jit(solution)/shard_map/all_to_all | solution.py:71
  53.8 20.8 %copy-start = (f32[27,8,1]{0,1,2:T(8,128)S(1)}, f32[27,8,1]{0,1,2:T(8,128)}, u32[]{:S(2)}) copy-start(f32[27,8,1]{0,1,2:T(8,128)} %constant.39) | copy-start | bytes 2596
  53.8 18.4 %all-to-all-start = ((f32[4,32,8,128]{3,0,2,1:T(4,128)}), f32[4,32,8,128]{3,0,2,1:T(4,128)S(1)}, u32[]{:S(2)}, u32[]{:S(2)}) async-start(f32[4,32,8,128]{3,0,2,1:T(4,128)} %bitcast.8), calls=%async_computation | async-start | bytes 1048576 | tf_op jit(solution)/shard_map/all_to_all | solution.py:70
